TPU v7x, 32 devices: a whole 2x2x4 slice. The times are simulated.
32 devices in a mesh: tm: 8 (over z, core), member: 4 (over y, x).
Axes of the slice: x: 2, y: 2, z: 4, core: 2. Of those that a mesh axis runs over, the one named last changes fastest.
Arguments:
- fields: float32 [48, 48, 8192], P('member', 'tm'), may hold values from 200 to 350, as said below
Outputs:
- covariance: float32 [48, 48, 8192], P('member', None, 'tm')
Inputs may be any that keep to these rules, and one draw needn't show every extreme that they name: `fields`: month t is calendar month t mod 12.
All inputs are finite; a program needn't handle non-finite values.
Results may differ from a plain program's by a relative error of at most 0.0003.
Values sent between devices are 32-bit elements; how exact they have to be, the bound alone decides.
A program may use at most 192 MiB of HBM per device.

v0:
```python
import jax
import jax.numpy as jnp
from jax import lax
from jax.sharding import PartitionSpec as P


def monthly_anomaly(series):
    members_here, months_here, pixel_count = series.shape
    by_year = series.reshape(members_here, months_here // 12, 12, pixel_count)
    climatology = jnp.mean(by_year, axis=1, keepdims=True)
    return (by_year - climatology).reshape(members_here, months_here, pixel_count)


def cross_block(first_rows, second_rows, divisor):
    products = jnp.einsum(
        "itp,jtp->ijp",
        first_rows,
        second_rows,
        precision=lax.Precision.HIGHEST,
        preferred_element_type=jnp.float32,
    )
    return products / divisor


def per_device(fields):
    members_here, mon_here, pixel_count = fields.shape
    tm_count = lax.axis_size("tm")
    divisor = float(mon_here * tm_count - 12)
    regrouped = lax.all_to_all(
        lax.all_to_all(fields, "tm", split_axis=2, concat_axis=1, tiled=True),
        "member",
        split_axis=2,
        concat_axis=0,
        tiled=True,
    )
    anomaly = monthly_anomaly(regrouped)
    whole_block = cross_block(anomaly, anomaly, divisor)
    return lax.all_to_all(whole_block, "member", split_axis=0, concat_axis=2, tiled=True)


def solution(mesh):
    in_specs = (P("member", "tm", None),)
    out_specs = P("member", None, "tm")
    return jax.shard_map(
        per_device, mesh=mesh, in_specs=in_specs, out_specs=out_specs, check_vma=False
    )
```

profile of v0, /device:TPU:0, one launch (start us, length us, event | category | flops | bytes accessed | tf_op | source)
XLA Modules:
  0.0 288.6 jit_solution(1620361578068104155)
XLA Ops:
  0.0 17.2 %copy.42 = f32[12,6,8192]{0,1,2:T(8,128)} copy(f32[12,6,8192]{2,1,0:T(8,128)} %param.1) | data formatting | bytes 4718592 | tf_op args[0]
  17.2 18.9 %reshape.15 = f32[8,1,73728]{2,1,0:T(1,128)S(1)} reshape(f32[8192,6,12]{2,1,0:T(8,128)} %bitcast.24) | data formatting | bytes 4718592
  36.2 60.9 %all_to_all.51 = f32[8,1,73728]{2,1,0:T(1,128)} all-to-all(f32[8,1,73728]{2,1,0:T(1,128)S(1)} %reshape.15), channel_id=1, replica_groups=mesh['tm'=8,'member'=4] {'tm'}, dimensions={0} | all-to-all | bytes 4718592 | tf_op jit(solution)/shard_map/all_to_all | solution.py:30
  97.1 0.6 broadcast.10
  97.6 7.9 %reduce.1 = f32[8,73728]{1,0:T(8,128)S(1)} reduce(f32[8,1,73728]{2,1,0:T(1,128)} %all_to_all.51, f32[]{:T(128)} %broadcast.10), dimensions={1}, to_apply=%all_to_all.37.reduce_sub_computation | reduce | bytes 4718596 | tf_op jit(solution)/shard_map/all_to_all | solution.py:30
  105.6 26.8 %reshape.16 = f32[8192,6,12]{2,1,0:T(8,128)} reshape(f32[8,73728]{1,0:T(8,128)S(1)} %reduce.1) | data formatting | bytes 4718592
  132.4 19.7 %copy.43 = f32[12,6,8,1024]{3,1,2,0:T(8,128)S(1)} copy(f32[12,6,8,1024]{0,1,3,2:T(8,128)} %bitcast.23) | data formatting | bytes 4718592 | tf_op jit(solution)/shard_map/all_to_all | solution.py:30
  152.1 1.6 all_to_all.40
  153.7 7.6 %copy.44 = f32[12,48,1024]{1,0,2:T(8,128)} copy(f32[12,48,1024]{2,1,0:T(8,128)} %all_to_all.40) | data formatting | bytes 4718592 | tf_op jit(solution)/shard_map/all_to_all | solution.py:30
  161.2 8.8 %reshape.17 = f32[4,1,147456]{2,1,0:T(1,128)} reshape(f32[1024,12,48]{2,1,0:T(8,128)} %bitcast.25) | data formatting | bytes 4718592
  170.0 31.9 %all_to_all.52 = f32[4,1,147456]{2,1,0:T(1,128)S(1)} all-to-all(f32[4,1,147456]{2,1,0:T(1,128)} %reshape.17), channel_id=1, replica_groups=mesh['tm'=8,'member'=4] {'member'}, dimensions={0} | all-to-all | bytes 4718592 | tf_op jit(solution)/shard_map/all_to_all | solution.py:29
  201.9 8.3 %reduce.2 = f32[4,147456]{1,0:T(4,128)} reduce(f32[4,1,147456]{2,1,0:T(1,128)S(1)} %all_to_all.52, f32[]{:T(128)} %broadcast.10), dimensions={1}, to_apply=%all_to_all.41.reduce_sub_computation | reduce | bytes 4718596 | tf_op jit(solution)/shard_map/all_to_all | solution.py:29
  210.2 10.3 %reshape.18 = f32[1024,12,48]{2,1,0:T(8,128)} reshape(f32[4,147456]{1,0:T(4,128)} %reduce.2) | data formatting | bytes 4718592
  220.5 5.7 %copy.54 = f32[12,48,4,256]{3,2,1,0:T(4,128)S(1)} copy(f32[12,48,4,256]{1,0,3,2:T(8,128)} %bitcast.26) | data formatting | bytes 4718592 | tf_op jit(solution)/shard_map/all_to_all | solution.py:29
  226.2 0.8 reduce
  226.9 0.1 copy.55
  227.1 0.4 copy_multiply_fusion
  227.5 0.5 copy.46
  227.9 0.3 sub.11
  228.2 1.4 bitcast_subtract_fusion
  229.6 5.4 %copy.50 = f32[48,48,256]{1,0,2:T(8,128)} copy(f32[48,48,256]{2,1,0:T(8,128)S(1)} %bitcast_subtract_fusion) | data formatting | bytes 4718592 | tf_op jit(solution)/shard_map/sub | solution.py:11
  235.1 16.4 %multiply_bitcast_fusion = f32[48,48,256]{0,1,2:T(8,128)} fusion(f32[48,48,256]{1,0,2:T(8,128)} %copy.50), kind=kOutput, calls=%fused_computation | convolution fusion | flops 340328448 | bytes 4718592 | tf_op jit(solution)/shard_map/itp,jtp->ijp/dot_general | solution.py:15
  251.5 5.9 %copy.52 = f32[48,48,256]{2,1,0:T(8,128)S(1)} copy(f32[48,48,256]{0,1,2:T(8,128)} %multiply_bitcast_fusion) | data formatting | bytes 4718592 | tf_op jit(solution)/shard_map/div | solution.py:22
  257.3 29.3 %all_to_all.53 = f32[48,48,256]{2,1,0:T(8,128)S(1)} all-to-all(f32[48,48,256]{2,1,0:T(8,128)S(1)} %copy.52), channel_id=1, replica_groups=mesh['tm'=8,'member'=4] {'member'}, dimensions={0} | all-to-all | bytes 4718592 | tf_op jit(solution)/shard_map/all_to_all | solution.py:38
  286.6 1.7 copy.56
where the time goes:
time: 293 us; the launch traced here: 289 us
  local copies, waits for them, and re-layouts  131 us (45%)
  blocking collectives  122 us (42%)
  other arithmetic  18.8 us (6%)
  matrix products  16.4 us (6%)
    unnamed x6, local copies, waits for them, and re-layouts  82.1 us
    all_to_all x1, blocking collectives, per_device(): lax.all_to_all(fields, 'tm', split_axis=2, concat_axis=1, tiled=True)  60.9 us
    all_to_all x1, blocking collectives, per_device(): lax.all_to_all(lax.all_to_all(fields, 'tm', split_axis=2, concat_axis=1,...  31.9 us
    all_to_all x4, local copies, waits for them, and re-layouts, per_device(): lax.all_to_all(fields, 'tm', split_axis=2, concat_axis=1, tiled=True)  29.4 us
    all_to_all x1, blocking collectives, per_device(): lax.all_to_all(whole_block, 'member', split_axis=0, concat_axis=2, tiled=...  29.3 us
    dot_general x1, matrix products, cross_block(): jnp.einsum('itp,jtp->ijp', first_rows, second_rows, precision=lax.Precisi...  16.4 us
    all_to_all x1, other arithmetic, per_device(): lax.all_to_all(lax.all_to_all(fields, 'tm', split_axis=2, concat_axis=1,...  8.3 us
    all_to_all x1, other arithmetic, per_device(): lax.all_to_all(fields, 'tm', split_axis=2, concat_axis=1, tiled=True)  7.95 us

commit v1 on v0

--- a/solution.py
+++ b/solution.py
@@ -35,7 +35,12 @@
     )
     anomaly = monthly_anomaly(regrouped)
     whole_block = cross_block(anomaly, anomaly, divisor)
-    return lax.all_to_all(whole_block, "member", split_axis=0, concat_axis=2, tiled=True)
+    return jnp.concatenate(
+        lax.all_to_all(
+            jnp.stack(jnp.split(whole_block, lax.axis_size("member"), axis=0)), "member", 0, 0
+        ),
+        axis=2,
+    )
 
 
 def solution(mesh):

time: 293 us -> 299 us (1.020)
  local copies, waits for them, and re-layouts: 131 us -> 137 us
    another operation x0 -> x5, local copies, waits for them, and re-layouts: none -> 12.2 us  [per_device(): jnp.stack(jnp.split(whole_block, lax.axis_size('member'), axis=0))]
    div x1 -> x0, local copies, waits for them, and re-layouts: 5.86 us -> none  [cross_block(): return products / divisor]
where the time goes in v1:
time: 299 us; the launch traced here: 295 us
  local copies, waits for them, and re-layouts  137 us (46%)
  blocking collectives  122 us (41%)
  other arithmetic  20.2 us (7%)
  matrix products  15.3 us (5%)
    unnamed x6, local copies, waits for them, and re-layouts  82.2 us
    all_to_all x1, blocking collectives, per_device(): lax.all_to_all(fields, 'tm', split_axis=2, concat_axis=1, tiled=True)  60.9 us
    all_to_all x1, blocking collectives, per_device(): lax.all_to_all(lax.all_to_all(fields, 'tm', split_axis=2, concat_axis=1,...  32.1 us
    all_to_all x4, local copies, waits for them, and re-layouts, per_device(): lax.all_to_all(fields, 'tm', split_axis=2, concat_axis=1, tiled=True)  29.4 us
    all_to_all x1, blocking collectives, per_device(): lax.all_to_all(jnp.stack(jnp.split(whole_block, lax.axis_size('member'),...  29.3 us
    dot_general x1, matrix products, cross_block(): jnp.einsum('itp,jtp->ijp', first_rows, second_rows, precision=lax.Precisi...  15.3 us
    another operation x5, local copies, waits for them, and re-layouts, per_device(): jnp.stack(jnp.split(whole_block, lax.axis_size('member'), axis=0))  12.2 us
    all_to_all x1, other arithmetic, per_device(): lax.all_to_all(lax.all_to_all(fields, 'tm', split_axis=2, concat_axis=1,...  8.3 us

profile of v1, /device:TPU:0, one launch (start us, length us, event | category | flops | bytes accessed | tf_op | source)
XLA Modules:
  0.0 295.2 jit_solution(9769551122418458646)
XLA Ops:
  0.0 17.2 %copy.54 = f32[12,6,8192]{0,1,2:T(8,128)} copy(f32[12,6,8192]{2,1,0:T(8,128)} %param.1) | data formatting | bytes 4718592 | tf_op args[0]
  17.2 18.9 %reshape.23 = f32[8,1,73728]{2,1,0:T(1,128)S(1)} reshape(f32[8192,6,12]{2,1,0:T(8,128)} %bitcast.30) | data formatting | bytes 4718592
  36.2 60.9 %all_to_all.38 = f32[8,1,73728]{2,1,0:T(1,128)} all-to-all(f32[8,1,73728]{2,1,0:T(1,128)S(1)} %reshape.23), channel_id=1, replica_groups=mesh['tm'=8,'member'=4] {'tm'}, dimensions={0} | all-to-all | bytes 4718592 | tf_op jit(solution)/shard_map/all_to_all | solution.py:30
  97.1 0.6 broadcast.10
  97.6 7.9 %reduce.1 = f32[8,73728]{1,0:T(8,128)S(1)} reduce(f32[8,1,73728]{2,1,0:T(1,128)} %all_to_all.38, f32[]{:T(128)} %broadcast.10), dimensions={1}, to_apply=%all_to_all.27.reduce_sub_computation | reduce | bytes 4718596 | tf_op jit(solution)/shard_map/all_to_all | solution.py:30
  105.6 26.9 %reshape.24 = f32[8192,6,12]{2,1,0:T(8,128)} reshape(f32[8,73728]{1,0:T(8,128)S(1)} %reduce.1) | data formatting | bytes 4718592
  132.4 19.7 %copy.55 = f32[12,6,8,1024]{3,1,2,0:T(8,128)S(1)} copy(f32[12,6,8,1024]{0,1,3,2:T(8,128)} %bitcast.29) | data formatting | bytes 4718592 | tf_op jit(solution)/shard_map/all_to_all | solution.py:30
  152.1 1.6 all_to_all.30
  153.7 7.6 %copy.56 = f32[12,48,1024]{1,0,2:T(8,128)} copy(f32[12,48,1024]{2,1,0:T(8,128)} %all_to_all.30) | data formatting | bytes 4718592 | tf_op jit(solution)/shard_map/all_to_all | solution.py:30
  161.3 8.8 %reshape.25 = f32[4,1,147456]{2,1,0:T(1,128)} reshape(f32[1024,12,48]{2,1,0:T(8,128)} %bitcast.31) | data formatting | bytes 4718592
  170.1 32.1 %all_to_all.39 = f32[4,1,147456]{2,1,0:T(1,128)S(1)} all-to-all(f32[4,1,147456]{2,1,0:T(1,128)} %reshape.25), channel_id=1, replica_groups=mesh['tm'=8,'member'=4] {'member'}, dimensions={0} | all-to-all | bytes 4718592 | tf_op jit(solution)/shard_map/all_to_all | solution.py:29
  202.1 8.3 %reduce.2 = f32[4,147456]{1,0:T(4,128)} reduce(f32[4,1,147456]{2,1,0:T(1,128)S(1)} %all_to_all.39, f32[]{:T(128)} %broadcast.10), dimensions={1}, to_apply=%all_to_all.31.reduce_sub_computation | reduce | bytes 4718596 | tf_op jit(solution)/shard_map/all_to_all | solution.py:29
  210.4 10.3 %reshape.26 = f32[1024,12,48]{2,1,0:T(8,128)} reshape(f32[4,147456]{1,0:T(4,128)} %reduce.2) | data formatting | bytes 4718592
  220.7 5.7 %copy.69 = f32[12,48,4,256]{3,2,1,0:T(4,128)S(1)} copy(f32[12,48,4,256]{1,0,3,2:T(8,128)} %bitcast.32) | data formatting | bytes 4718592 | tf_op jit(solution)/shard_map/all_to_all | solution.py:29
  226.4 0.8 reduce
  227.2 0.1 copy.70
  227.3 0.4 copy_multiply_fusion
  227.7 0.5 copy.58
  228.2 0.3 sub.11
  228.4 1.4 bitcast_subtract_fusion
  229.9 5.4 %copy.62 = f32[48,48,256]{1,0,2:T(8,128)} copy(f32[48,48,256]{2,1,0:T(8,128)S(1)} %bitcast_subtract_fusion) | data formatting | bytes 4718592 | tf_op jit(solution)/shard_map/sub | solution.py:11
  235.2 15.3 %multiply_bitcast_fusion = f32[48,48,256]{1,0,2:T(8,128)S(1)} fusion(f32[48,48,256]{1,0,2:T(8,128)} %copy.62), kind=kOutput, calls=%fused_computation | convolution fusion | flops 340328448 | bytes 4718592 | tf_op jit(solution)/shard_map/itp,jtp->ijp/dot_general | solution.py:15
  250.5 2.9 slice_bitcast_fusion.3
  253.4 2.3 copy.64
  255.7 2.3 copy.67
  258.0 3.1 %copy.66 = f32[1,12,48,256]{3,2,1,0:T(8,128)} copy(f32[1,12,48,256]{2,1,3,0:T(8,128)} %get-tuple-element.7) | data formatting | bytes 1179648 | tf_op jit(solution)/shard_map/stack | solution.py:40
  261.1 1.6 copy.65
  262.7 1.4 pad_maximum_fusion
  264.1 29.3 %all_to_all.40 = f32[4,12,48,256]{3,2,1,0:T(8,128)S(1)} all-to-all(f32[4,12,48,256]{3,2,1,0:T(8,128)S(1)} %pad_maximum_fusion), channel_id=1, replica_groups=mesh['tm'=8,'member'=4] {'member'}, dimensions={0} | all-to-all | bytes 4718592 | tf_op jit(solution)/shard_map/all_to_all | solution.py:39
  293.4 1.7 copy.71

commit v2 on v0

--- a/solution.py
+++ b/solution.py
@@ -26,12 +26,20 @@
     members_here, mon_here, pixel_count = fields.shape
     tm_count = lax.axis_size("tm")
     divisor = float(mon_here * tm_count - 12)
-    regrouped = lax.all_to_all(
-        lax.all_to_all(fields, "tm", split_axis=2, concat_axis=1, tiled=True),
-        "member",
-        split_axis=2,
-        concat_axis=0,
-        tiled=True,
+    regrouped = jnp.concatenate(
+        lax.all_to_all(
+            jnp.stack(
+                jnp.split(
+                    lax.all_to_all(fields, "tm", split_axis=2, concat_axis=1, tiled=True),
+                    lax.axis_size("member"),
+                    axis=2,
+                )
+            ),
+            "member",
+            0,
+            0,
+        ),
+        axis=0,
     )
     anomaly = monthly_anomaly(regrouped)
     whole_block = cross_block(anomaly, anomaly, divisor)

time: 293 us -> 255 us (0.87); the launches traced: 289 us -> 254 us
  local copies, waits for them, and re-layouts: 131 us -> 103 us
  other arithmetic: 18.8 us -> 13.7 us
    unnamed x6 -> x3, local copies, waits for them, and re-layouts: 82.1 us -> 63 us
    all_to_all x1 -> x0, other arithmetic: 8.3 us -> none  [per_device(): lax.all_to_all(lax.all_to_all(fields, 'tm', split_axis=2, concat_axis=1,...]
    all_to_all x4 -> x3, local copies, waits for them, and re-layouts: 29.4 us -> 21.8 us  [per_device(): lax.all_to_all(fields, 'tm', split_axis=2, concat_axis=1, tiled=True)]
    all_to_all x2 -> x0, local copies, waits for them, and re-layouts: 6.12 us -> none  [per_device(): lax.all_to_all(lax.all_to_all(fields, 'tm', split_axis=2, concat_axis=1,...]
    another operation x0 -> x2, local copies, waits for them, and re-layouts: none -> 3.56 us  [the longest x1 1.79 us: monthly_anomaly(): by_year = series.reshape(members_here, months_here // 12, 12, pixel_count)]
where the time goes in v2:
time: 255 us; the launch traced here: 254 us
  blocking collectives  121 us (47%)
  local copies, waits for them, and re-layouts  103 us (40%)
  matrix products  16.4 us (6%)
  other arithmetic  13.7 us (5%)
    unnamed x3, local copies, waits for them, and re-layouts  63 us
    all_to_all x1, blocking collectives, per_device(): lax.all_to_all(fields, 'tm', split_axis=2, concat_axis=1, tiled=True)  60.9 us
    all_to_all x1, blocking collectives, per_device(): lax.all_to_all(jnp.stack(jnp.split(lax.all_to_all(fields, 'tm', split_axi...  31.3 us
    all_to_all x1, blocking collectives, per_device(): lax.all_to_all(whole_block, 'member', split_axis=0, concat_axis=2, tiled=...  28.9 us
    all_to_all x3, local copies, waits for them, and re-layouts, per_device(): lax.all_to_all(fields, 'tm', split_axis=2, concat_axis=1, tiled=True)  21.8 us
    dot_general x1, matrix products, cross_block(): jnp.einsum('itp,jtp->ijp', first_rows, second_rows, precision=lax.Precisi...  16.4 us
    all_to_all x1, other arithmetic, per_device(): lax.all_to_all(fields, 'tm', split_axis=2, concat_axis=1, tiled=True)  7.92 us
    sub x2, local copies, waits for them, and re-layouts, monthly_anomaly(): by_year - climatology  6.75 us

profile of v2, /device:TPU:0, one launch (start us, length us, event | category | flops | bytes accessed | tf_op | source)
XLA Modules:
  0.0 253.9 jit_solution(16869253612356793761)
XLA Ops:
  0.0 17.2 %copy.33 = f32[12,6,8192]{0,1,2:T(8,128)} copy(f32[12,6,8192]{2,1,0:T(8,128)} %param.1) | data formatting | bytes 4718592 | tf_op args[0]
  17.2 18.9 %reshape.7 = f32[8,1,73728]{2,1,0:T(1,128)S(1)} reshape(f32[8192,6,12]{2,1,0:T(8,128)} %bitcast.27) | data formatting | bytes 4718592
  36.2 60.9 %all_to_all.41 = f32[8,1,73728]{2,1,0:T(1,128)} all-to-all(f32[8,1,73728]{2,1,0:T(1,128)S(1)} %reshape.7), channel_id=1, replica_groups=mesh['tm'=8,'member'=4] {'tm'}, dimensions={0} | all-to-all | bytes 4718592 | tf_op jit(solution)/shard_map/all_to_all | solution.py:33
  97.1 0.5 broadcast.10
  97.6 7.9 %reduce = f32[8,73728]{1,0:T(8,128)S(1)} reduce(f32[8,1,73728]{2,1,0:T(1,128)} %all_to_all.41, f32[]{:T(128)} %broadcast.10), dimensions={1}, to_apply=%all_to_all.29.reduce_sub_computation | reduce | bytes 4718596 | tf_op jit(solution)/shard_map/all_to_all | solution.py:33
  105.5 26.9 %reshape.8 = f32[8192,6,12]{2,1,0:T(8,128)} reshape(f32[8,73728]{1,0:T(8,128)S(1)} %reduce) | data formatting | bytes 4718592
  132.4 19.7 %copy.34 = f32[12,6,8,1024]{3,1,2,0:T(8,128)S(1)} copy(f32[12,6,8,1024]{0,1,3,2:T(8,128)} %bitcast.26) | data formatting | bytes 4718592 | tf_op jit(solution)/shard_map/all_to_all | solution.py:33
  152.0 1.6 all_to_all.32
  153.6 1.8 slice_bitcast_fusion.3
  155.4 0.2 pad_maximum_fusion
  155.6 31.3 %all_to_all.42 = f32[4,12,48,256]{3,2,1,0:T(8,128)S(1)} all-to-all(f32[4,12,48,256]{3,2,1,0:T(8,128)S(1)} %pad_maximum_fusion), channel_id=1, replica_groups=mesh['tm'=8,'member'=4] {'member'}, dimensions={0} | all-to-all | bytes 4718592 | tf_op jit(solution)/shard_map/all_to_all | solution.py:30
  186.9 1.8 reshape_reshape.6
  188.7 2.4 reduce_sum.9
  191.1 0.4 copy_multiply_fusion
  191.4 0.3 sub.11
  191.7 2.8 %bitcast_subtract_fusion = f32[48,48,256]{2,1,0:T(8,128)} fusion(f32[4,12,48,256]{3,2,1,0:T(8,128)S(1)} %all_to_all.42, f32[48,48,256]{2,0,1:T(8,128)S(1)} %bitcast.29), kind=kLoop, calls=%fused_computation.2 | loop fusion | flops 589824 | bytes 7077888 | tf_op jit(solution)/shard_map/sub | solution.py:11
  194.6 6.5 %copy.37 = f32[48,48,256]{1,0,2:T(8,128)} copy(f32[48,48,256]{2,1,0:T(8,128)} %bitcast_subtract_fusion) | data formatting | bytes 4718592 | tf_op jit(solution)/shard_map/sub | solution.py:11
  201.0 16.4 %multiply_bitcast_fusion = f32[48,48,256]{0,1,2:T(8,128)} fusion(f32[48,48,256]{1,0,2:T(8,128)} %copy.37), kind=kOutput, calls=%fused_computation | convolution fusion | flops 340328448 | bytes 4718592 | tf_op jit(solution)/shard_map/itp,jtp->ijp/dot_general | solution.py:15
  217.4 5.9 %copy.39 = f32[48,48,256]{2,1,0:T(8,128)S(1)} copy(f32[48,48,256]{0,1,2:T(8,128)} %multiply_bitcast_fusion) | data formatting | bytes 4718592 | tf_op jit(solution)/shard_map/div | solution.py:22
  223.3 28.9 %all_to_all.43 = f32[48,48,256]{2,1,0:T(8,128)S(1)} all-to-all(f32[48,48,256]{2,1,0:T(8,128)S(1)} %copy.39), channel_id=1, replica_groups=mesh['tm'=8,'member'=4] {'member'}, dimensions={0} | all-to-all | bytes 4718592 | tf_op jit(solution)/shard_map/all_to_all | solution.py:46
  252.2 1.7 copy.41
